TPU v7x, 256 devices: a whole 4x4x8 slice. The times are simulated.
256 devices in a mesh: pop: 32 (over z, y_lo, core), tp: 8 (over y_hi, x).
Axes of the slice: x: 4, y: 4 (y_hi: 2, y_lo: 2; y = y_hi * 2 + y_lo), z: 8, core: 2. Of those that a mesh axis runs over, the one named last changes fastest.
Arguments:
- tokens: bfloat16 [32, 512, 1792], P('pop', None, 'tp'), may hold values from -6 to 6
- weight: bfloat16 [32, 1792, 7168], P('pop', 'tp'), may hold values from -0.125 to 0.125
- momentum: bfloat16 [32, 1792, 7168], P('pop', 'tp'), may hold values from -6 to 6
- cotangent: bfloat16 [32, 512, 7168], P('pop', None, 'tp'), may hold values from -0.5 to 0.5
- assignment: int32 [8, 2], replicated, may hold values from 0 to 31, as said below
- lr_index: int32 [32], replicated, may hold values from 0 to 7
- rates: float32 [8], replicated, may hold values from 0.01 to 0.1
Outputs:
- activation: bfloat16 [32, 512, 7168], P('pop', None, 'tp')
- new_weight: bfloat16 [32, 1792, 7168], P('pop', 'tp')
Inputs may be any that keep to these rules, and one draw needn't show every extreme that they name: `assignment`: column 0 names 8 distinct members; column 1 names exactly 2 distinct members, each in some row, none of them in column 0.
All inputs are finite; a program needn't handle non-finite values.
Results may differ from a plain program's by a relative error of at most 0.015.
Values may be sent and summed in bfloat16 or wider, within the bound.
No kernel may reach another device: no remote copies, remote signals or barrier semaphores. Data moves between devices by JAX's collectives and lax.ppermute only.
A program may use at most 192 MiB of HBM per device.

v0:
```python
import jax
import jax.numpy as jnp
from jax import lax
from jax.sharding import PartitionSpec as P


def side_by_side(arrays, axis, split_dim, concat_dim, along):
    both = jnp.concatenate(arrays, axis=along)
    filled, at, done = (
        lax.all_to_all(both, axis, split_axis=split_dim, concat_axis=concat_dim, tiled=True),
        0,
        [],
    )
    for a in arrays:
        done.append(lax.slice_in_dim(filled, at, at + a.shape[along], axis=along))
        at += a.shape[along]
    return tuple(done)


def gelu_tanh(value):
    return jax.nn.gelu(value, approximate=True)


def activate(hidden, cot_block):
    active, pullback = jax.vjp(gelu_tanh, hidden)
    grad_hidden = pullback(cot_block.astype(jnp.float32))[0].astype(jnp.bfloat16)
    return (active.astype(jnp.bfloat16), grad_hidden)


def local(tokens, weight, momentum, cotangent, assignment, lr_index, rates):
    members = lax.axis_size("pop")
    me = lax.axis_index("pop")
    member_ids = jnp.arange(members, dtype=jnp.int32)
    hit = assignment[:, 0][None, :] == member_ids[:, None]
    source_all = jnp.where(
        jnp.any(hit, axis=1),
        jnp.sum(jnp.where(hit, assignment[:, 1][None, :], 0), axis=1),
        member_ids,
    )
    my_index = jnp.sum(jnp.where(member_ids == me, lr_index, 0))
    rate_ids = jnp.arange(rates.shape[0], dtype=jnp.int32)
    my_rate = jnp.sum(jnp.where(rate_ids == my_index, rates, 0.0))
    flat_weight = weight.reshape(members, -1)
    flat_momentum = momentum.reshape(members, -1)
    held = side_by_side((flat_weight, flat_momentum), "pop", 0, 0, 1)
    picked = (held[0][source_all], held[1][source_all])
    returned = side_by_side((picked[0], picked[1]), "pop", 0, 0, 1)
    taken_weight = returned[0].reshape(weight.shape)[0]
    taken_momentum = returned[1].reshape(momentum.shape)[0]
    inputs = tokens[0]
    partial_value = jnp.dot(inputs, taken_weight, preferred_element_type=jnp.float32)
    hidden_share = lax.psum_scatter(
        partial_value.astype(jnp.bfloat16), "tp", scatter_dimension=1, tiled=True
    ).astype(jnp.float32)
    activation, grad_share = activate(hidden_share, cotangent[0])
    grad_hidden = lax.all_gather(grad_share, "tp", axis=1, tiled=True)
    grad_weight = lax.dot_general(
        inputs, grad_hidden, (((0,), (0,)), ((), ())), preferred_element_type=jnp.float32
    )
    new_momentum = 0.9 * taken_momentum.astype(jnp.float32) + grad_weight
    updated = (taken_weight.astype(jnp.float32) - my_rate * new_momentum).astype(jnp.bfloat16)
    return (activation[None], updated[None])


def solution(mesh):
    placed = (
        P("pop", None, "tp"),
        P("pop", "tp", None),
        P("pop", "tp", None),
        P("pop", None, "tp"),
        P(),
        P(),
        P(),
    )
    return jax.shard_map(
        local,
        mesh=mesh,
        in_specs=placed,
        out_specs=(P("pop", None, "tp"), P("pop", "tp", None)),
        check_vma=False,
    )
```

profile of v0, /device:TPU:1, one launch (start us, length us, event | category | flops | bytes accessed | tf_op | source)
XLA Modules:
  0.0 701.8 jit_solution(3552922835400282896)
XLA Ops:
  7.2 0.0 copy-start
  7.2 5.6 reshape.46
  12.8 6.7 reshape.45
  19.5 5.0 maximum_bitcast_fusion
  24.5 0.5 broadcast.61
  25.0 9.3 %reduce = bf16[32,100352]{1,0:T(8,128)(2,1)} reduce(bf16[32,1,100352]{2,0,1:T(8,128)(2,1)} %maximum_bitcast_fusion, bf16[]{:T(256)} %broadcast.61), dimensions={1}, to_apply=%copy.18.reduce_sub_computation | reduce | bytes 12845058 | tf_op jit(solution)/shard_map/all_to_all | solution.py:10
  34.4 8.9 %reshape.64 = bf16[32,2,50176]{2,1,0:T(2,128)(2,1)} reshape(bf16[32,100352]{1,0:T(8,128)(2,1)} %reduce) | data formatting | bytes 12845056
  43.2 0.0 copy-start.1
  43.2 11.3 %all-to-all-start = ((bf16[32,2,50176]{2,1,0:T(2,128)(2,1)}), bf16[32,2,50176]{2,1,0:T(2,128)(2,1)}, u32[]{:S(2)}, u32[]{:S(2)}) async-start(bf16[32,2,50176]{2,1,0:T(2,128)(2,1)} %reshape.64), calls=%async_computation | async-start | bytes 12845056 | tf_op jit(solution)/shard_map/all_to_all | solution.py:10
  54.5 0.0 reduce-scatter.2.cloned.1.call-start
  54.6 0.0 copy-done.1
  54.6 0.1 fusion.20
  54.7 0.1 select_reduce_fusion
  54.8 141.1 %all-to-all-done = bf16[32,2,50176]{2,1,0:T(2,128)(2,1)} async-done(((bf16[32,2,50176]{2,1,0:T(2,128)(2,1)}), bf16[32,2,50176]{2,1,0:T(2,128)(2,1)}, u32[]{:S(2)}, u32[]{:S(2)}) %all-to-all-start) | async-done | bytes 6422560 | tf_op jit(solution)/shard_map/all_to_all | solution.py:10
  195.9 21.7 %reshape.65 = bf16[32,1,100352]{2,1,0:T(2,128)(2,1)} reshape(bf16[32,2,50176]{2,1,0:T(2,128)(2,1)} %all-to-all-done) | data formatting | bytes 12845056
  217.7 11.0 %copy.27 = bf16[32,1,100352]{2,0,1:T(8,128)(2,1)} copy(bf16[32,1,100352]{2,1,0:T(2,128)(2,1)} %reshape.65) | data formatting | bytes 12845056
  228.7 5.0 fusion.24
  233.7 9.4 %gather_fusion.1 = bf16[32,50176]{1,0:T(8,128)(2,1)} fusion(bf16[32,50176]{1,0:T(8,128)(2,1)} %get-tuple-element.11, s32[1024]{0:T(1024)S(1)} %pad_clamp_fusion), kind=kCustom, calls=%fused_computation.1 | custom fusion | bytes 6422656 | tf_op jit(solution)/shard_map/gather | solution.py:46
  243.0 4.3 gather_fusion
  247.4 6.0 maximum_bitcast_fusion.1
  253.4 9.5 %reduce.1 = bf16[32,100352]{1,0:T(8,128)(2,1)} reduce(bf16[32,1,100352]{2,0,1:T(8,128)(2,1)} %maximum_bitcast_fusion.1, bf16[]{:T(256)} %broadcast.61), dimensions={1}, to_apply=%copy.19.reduce_sub_computation | reduce | bytes 12845058 | tf_op jit(solution)/shard_map/all_to_all | solution.py:10
  262.9 8.9 %reshape.66 = bf16[32,2,50176]{2,1,0:T(2,128)(2,1)} reshape(bf16[32,100352]{1,0:T(8,128)(2,1)} %reduce.1) | data formatting | bytes 12845056
  271.7 151.7 %all_to_all.24 = bf16[32,2,50176]{2,1,0:T(2,128)(2,1)} all-to-all(bf16[32,2,50176]{2,1,0:T(2,128)(2,1)} %reshape.66), channel_id=1, replica_groups=mesh['pop'=32,'tp'=8] {'pop'}, dimensions={0} | all-to-all | bytes 12845056 | tf_op jit(solution)/shard_map/all_to_all | solution.py:10
  423.5 21.3 %reshape.67 = bf16[32,1,100352]{2,1,0:T(2,128)(2,1)} reshape(bf16[32,2,50176]{2,1,0:T(2,128)(2,1)} %all_to_all.24) | data formatting | bytes 12845056
  444.7 11.1 %copy.26 = bf16[32,1,100352]{2,0,1:T(8,128)(2,1)} copy(bf16[32,1,100352]{2,1,0:T(2,128)(2,1)} %reshape.67) | data formatting | bytes 12845056
  455.8 3.8 slice.30
  459.6 5.5 squeeze_reshape.4
  465.1 0.0 copy-done
  465.1 5.1 fusion
  470.3 0.0 reduce-scatter.2.cloned.1.call-update
  470.3 0.0 copy-start.2
  470.3 0.0 copy-start.3
  470.3 0.0 all-gather.2.cloned.1.call-start
  470.4 2.4 copy.20
  472.8 105.8 %reduce-scatter.2.cloned.1.call-done = bf16[512,896]{0,1:T(8,128)(2,1)} async-done(((bf16[512,7168]{0,1:T(8,128)(2,1)}), bf16[512,896]{0,1:T(8,128)(2,1)}) %reduce-scatter.2.cloned.1.call-update) | async-done | bytes 917520 | tf_op jit(solution)/shard_map/reduce_scatter | solution.py:52
  578.6 4.1 fusion.9
  582.8 0.0 all-gather.2.cloned.1.call-update
  582.8 0.0 copy-done.2
  582.8 0.6 fusion.21
  583.4 0.0 copy-done.3
  583.4 1.3 fusion.22
  584.7 5.0 convert_multiply_fusion
  589.7 6.3 mul.66
  596.1 2.3 copy.21
  598.4 86.8 %all-gather.2.cloned.1.call-done = bf16[512,7168]{0,1:T(8,128)(2,1)} async-done(((bf16[512,896]{0,1:T(8,128)(2,1)}), bf16[512,7168]{0,1:T(8,128)(2,1)}) %all-gather.2.cloned.1.call-update) | async-done | bytes 7340048 | tf_op jit(solution)/shard_map/all_gather | solution.py:56
  685.2 9.6 %fusion.5 = bf16[1,224,7168]{2,1,0:T(8,128)(2,1)} fusion(f32[224,7168]{1,0:T(8,128)} %mul.66, bf16[512,7168]{0,1:T(8,128)(2,1)} %all-gather.2.cloned.1.call-done, bf16[224,7168]{1,0:T(8,128)(2,1)S(1)} %squeeze_reshape.4, f32[]{:T(128)} %fusion.22, bf16[1,512,224]{1,2,0:T(8,128)(2,1)S(1)} %copy-done), kind=kOutput, calls=%fused_computation.9 | convolution fusion | flops 1652195328 | bytes 20414468 | tf_op jit(solution)/shard_map/dot_general | solution.py:57
  (3 shorter events, 0.0 us)
Async XLA Ops:
  7.2 458.0 %copy-start = (bf16[1,512,224]{1,2,0:T(8,128)(2,1)S(1)}, bf16[1,512,224]{1,2,0:T(8,128)(2,1)}, u32[]{:S(2)}) copy-start(bf16[1,512,224]{1,2,0:T(8,128)(2,1)} %param.7) | copy-start | bytes 688132
  43.2 11.4 %copy-start.1 = (s32[8,2]{0,1:T(2,128)S(1)}, s32[8,2]{0,1:T(2,128)}, u32[]{:S(2)}) copy-start(s32[8,2]{0,1:T(2,128)} %param.11) | copy-start | bytes 196
  43.2 152.7 %all-to-all-start = ((bf16[32,2,50176]{2,1,0:T(2,128)(2,1)}), bf16[32,2,50176]{2,1,0:T(2,128)(2,1)}, u32[]{:S(2)}, u32[]{:S(2)}) async-start(bf16[32,2,50176]{2,1,0:T(2,128)(2,1)} %reshape.64), calls=%async_computation | async-start | bytes 12845056 | tf_op jit(solution)/shard_map/all_to_all | solution.py:10
  54.5 524.1 %reduce-scatter.2.cloned.1.call-start = ((), (), s32[]{:S(2)}) async-start(), calls=%async_computation.3 | async-start | bytes 8257536 | tf_op jit(solution)/shard_map/reduce_scatter | solution.py:52
  470.3 112.5 %copy-start.2 = (s32[32]{0:T(128)S(1)}, s32[32]{0:T(128)}, u32[]{:S(2)}) copy-start(s32[32]{0:T(128)} %param.12) | copy-start | bytes 388
  470.3 113.1 %copy-start.3 = (f32[8]{0:T(128)S(1)}, f32[8]{0:T(128)}, u32[]{:S(2)}) copy-start(f32[8]{0:T(128)} %param.13) | copy-start | bytes 100
  470.3 214.8 %all-gather.2.cloned.1.call-start = ((), (), s32[]{:S(2)}) async-start(), calls=%async_computation.4 | async-start | bytes 8257536 | tf_op jit(solution)/shard_map/all_gather | solution.py:56
Sparse Core Ops, SparseCore 0:
  470.4 108.1 reduce-scatter.1
  582.9 102.2 all-gather.1
where the time goes:
time: 710 us; the launch traced here: 702 us
  waiting for transfers between devices  334 us (47%)
  blocking collectives  152 us (21%)
  local copies, waits for them, and re-layouts  135 us (19%)
  other arithmetic  41.1 us (6%)
  matrix products  14.7 us (2%)
  between operations  14.4 us (2%)
  starting transfers between devices  11.4 us (2%)
    all_to_all x1, blocking collectives, side_by_side(): lax.all_to_all(both, axis, split_axis=split_dim, concat_axis=concat_dim,...  152 us
    all_to_all x1, waiting for transfers between devices, side_by_side(): lax.all_to_all(both, axis, split_axis=split_dim, concat_axis=concat_dim,...  141 us
    reduce_scatter x1, waiting for transfers between devices, local(): lax.psum_scatter(partial_value.astype(jnp.bfloat16), 'tp', scatter_dimens...  106 us
    unnamed x16, local copies, waits for them, and re-layouts  87.6 us
    all_gather x1, waiting for transfers between devices, local(): grad_hidden = lax.all_gather(grad_share, 'tp', axis=1, tiled=True)  86.8 us
    all_to_all x4, other arithmetic, side_by_side(): lax.all_to_all(both, axis, split_axis=split_dim, concat_axis=concat_dim,...  29.8 us
  transfers between devices with their start and end apart: 3, of which 3 were waited for; matrix products, arithmetic and copies ran while one was open for 3% of the time, Pallas kernels for 0%

commit v1 on v0

--- a/solution.py
+++ b/solution.py
@@ -53,7 +53,9 @@
         partial_value.astype(jnp.bfloat16), "tp", scatter_dimension=1, tiled=True
     ).astype(jnp.float32)
     activation, grad_share = activate(hidden_share, cotangent[0])
-    grad_hidden = lax.all_gather(grad_share, "tp", axis=1, tiled=True)
+    grad_hidden = jnp.concatenate(
+        lax.all_to_all(jnp.stack([grad_share] * lax.axis_size("tp")), "tp", 0, 0), axis=1
+    )
     grad_weight = lax.dot_general(
         inputs, grad_hidden, (((0,), (0,)), ((), ())), preferred_element_type=jnp.float32
     )

time: 710 us -> 734 us (1.034)
  the two profiles are of different devices: /device:TPU:1 before, /device:TPU:6 now
where the time goes in v1:
time: 734 us; the launch traced here: 725 us
  waiting for transfers between devices  342 us (47%)
  blocking collectives  149 us (20%)
  local copies, waits for them, and re-layouts  138 us (19%)
  other arithmetic  51.5 us (7%)
  starting transfers between devices  16.3 us (2%)
  matrix products  14.7 us (2%)
  between operations  14.3 us (2%)
    all_to_all x1, blocking collectives, side_by_side(): lax.all_to_all(both, axis, split_axis=split_dim, concat_axis=concat_dim,...  149 us
    all_to_all x1, waiting for transfers between devices, side_by_side(): lax.all_to_all(both, axis, split_axis=split_dim, concat_axis=concat_dim,...  144 us
    reduce_scatter x1, waiting for transfers between devices, local(): lax.psum_scatter(partial_value.astype(jnp.bfloat16), 'tp', scatter_dimens...  104 us
    all_to_all x1, waiting for transfers between devices, local(): lax.all_to_all(jnp.stack([grad_share] * lax.axis_size('tp')), 'tp', 0, 0)  93.8 us
    unnamed x16, local copies, waits for them, and re-layouts  87.1 us
    all_to_all x4, other arithmetic, side_by_side(): lax.all_to_all(both, axis, split_axis=split_dim, concat_axis=concat_dim,...  40.4 us
  transfers between devices with their start and end apart: 3, of which 3 were waited for; matrix products, arithmetic and copies ran while one was open for 2% of the time, Pallas kernels for 0%

profile of v1, /device:TPU:6, one launch (start us, length us, event | category | flops | bytes accessed | tf_op | source)
XLA Modules:
  0.0 725.5 jit_solution(15653533331914912755)
XLA Ops:
  7.2 0.0 copy-start
  7.2 5.6 reshape.54
  12.8 6.7 reshape.53
  19.5 5.0 maximum_bitcast_fusion
  24.5 0.5 broadcast.63
  25.0 9.3 %reduce = bf16[32,100352]{1,0:T(8,128)(2,1)} reduce(bf16[32,1,100352]{2,0,1:T(8,128)(2,1)} %maximum_bitcast_fusion, bf16[]{:T(256)} %broadcast.63), dimensions={1}, to_apply=%copy.21.reduce_sub_computation | reduce | bytes 12845058 | tf_op jit(solution)/shard_map/all_to_all | solution.py:10
  34.4 8.9 %reshape.74 = bf16[32,2,50176]{2,1,0:T(2,128)(2,1)} reshape(bf16[32,100352]{1,0:T(8,128)(2,1)} %reduce) | data formatting | bytes 12845056
  43.2 0.0 copy-start.1
  43.2 10.1 %all-to-all-start = ((bf16[32,2,50176]{2,1,0:T(2,128)(2,1)}), bf16[32,2,50176]{2,1,0:T(2,128)(2,1)}, u32[]{:S(2)}, u32[]{:S(2)}) async-start(bf16[32,2,50176]{2,1,0:T(2,128)(2,1)} %reshape.74), calls=%async_computation | async-start | bytes 12845056 | tf_op jit(solution)/shard_map/all_to_all | solution.py:10
  53.3 0.0 reduce-scatter.2.cloned.1.call-start
  53.4 0.0 copy-done.1
  53.4 0.1 fusion.20
  53.5 0.1 select_reduce_fusion
  53.6 144.2 %all-to-all-done = bf16[32,2,50176]{2,1,0:T(2,128)(2,1)} async-done(((bf16[32,2,50176]{2,1,0:T(2,128)(2,1)}), bf16[32,2,50176]{2,1,0:T(2,128)(2,1)}, u32[]{:S(2)}, u32[]{:S(2)}) %all-to-all-start) | async-done | bytes 6422560 | tf_op jit(solution)/shard_map/all_to_all | solution.py:10
  197.8 21.7 %reshape.75 = bf16[32,1,100352]{2,1,0:T(2,128)(2,1)} reshape(bf16[32,2,50176]{2,1,0:T(2,128)(2,1)} %all-to-all-done) | data formatting | bytes 12845056
  219.5 11.0 %copy.30 = bf16[32,1,100352]{2,0,1:T(8,128)(2,1)} copy(bf16[32,1,100352]{2,1,0:T(2,128)(2,1)} %reshape.75) | data formatting | bytes 12845056
  230.5 5.0 fusion.24
  235.5 9.4 %gather_fusion.1 = bf16[32,50176]{1,0:T(8,128)(2,1)} fusion(bf16[32,50176]{1,0:T(8,128)(2,1)} %get-tuple-element.13, s32[1024]{0:T(1024)S(1)} %pad_clamp_fusion), kind=kCustom, calls=%fused_computation.1 | custom fusion | bytes 6422656 | tf_op jit(solution)/shard_map/gather | solution.py:46
  244.8 4.3 gather_fusion
  249.2 6.0 maximum_bitcast_fusion.1
  255.2 20.1 %reduce.1 = bf16[32,100352]{1,0:T(8,128)(2,1)} reduce(bf16[32,1,100352]{2,0,1:T(8,128)(2,1)} %maximum_bitcast_fusion.1, bf16[]{:T(256)} %broadcast.63), dimensions={1}, to_apply=%copy.22.reduce_sub_computation | reduce | bytes 12845058 | tf_op jit(solution)/shard_map/all_to_all | solution.py:10
  275.3 8.9 %reshape.76 = bf16[32,2,50176]{2,1,0:T(2,128)(2,1)} reshape(bf16[32,100352]{1,0:T(8,128)(2,1)} %reduce.1) | data formatting | bytes 12845056
  284.1 149.2 %all_to_all.29 = bf16[32,2,50176]{2,1,0:T(2,128)(2,1)} all-to-all(bf16[32,2,50176]{2,1,0:T(2,128)(2,1)} %reshape.76), channel_id=1, replica_groups=mesh['pop'=32,'tp'=8] {'pop'}, dimensions={0} | all-to-all | bytes 12845056 | tf_op jit(solution)/shard_map/all_to_all | solution.py:10
  433.4 21.3 %reshape.77 = bf16[32,1,100352]{2,1,0:T(2,128)(2,1)} reshape(bf16[32,2,50176]{2,1,0:T(2,128)(2,1)} %all_to_all.29) | data formatting | bytes 12845056
  454.7 11.0 %copy.29 = bf16[32,1,100352]{2,0,1:T(8,128)(2,1)} copy(bf16[32,1,100352]{2,1,0:T(2,128)(2,1)} %reshape.77) | data formatting | bytes 12845056
  465.7 3.8 slice.30
  469.5 5.5 squeeze_reshape.4
  475.0 0.0 copy-done
  475.0 5.1 fusion
  480.1 0.0 copy-start.2
  480.1 0.0 copy-start.3
  480.1 0.0 reduce-scatter.2.cloned.1.call-update
  480.1 2.2 copy.23
  482.3 0.0 copy-done.2
  482.3 0.6 fusion.21
  483.0 0.0 copy-done.3
  483.0 1.3 fusion.22
  484.3 103.6 %reduce-scatter.2.cloned.1.call-done = bf16[512,896]{0,1:T(8,128)(2,1)} async-done(((bf16[512,7168]{0,1:T(8,128)(2,1)}), bf16[512,896]{0,1:T(8,128)(2,1)}) %reduce-scatter.2.cloned.1.call-update) | async-done | bytes 917520 | tf_op jit(solution)/shard_map/reduce_scatter | solution.py:52
  587.9 3.8 fusion.9
  591.7 3.7 stack.2
  595.4 6.2 all-to-all-start.2
  601.5 5.1 convert_multiply_fusion
  606.6 6.2 mul.66
  612.8 2.2 copy.24
  615.0 93.8 %all-to-all-done.2 = bf16[8,512,896]{1,2,0:T(8,128)(2,1)} async-done(((bf16[8,512,896]{1,2,0:T(8,128)(2,1)}), bf16[8,512,896]{1,2,0:T(8,128)(2,1)}, u32[]{:S(2)}, u32[]{:S(2)}) %all-to-all-start.2) | async-done | bytes 7340064 | tf_op jit(solution)/shard_map/all_to_all | solution.py:57
  708.8 9.7 %fusion.5 = bf16[1,224,7168]{2,1,0:T(8,128)(2,1)} fusion(f32[224,7168]{1,0:T(8,128)} %mul.66, bf16[512,7168]{0,1:T(8,128)(2,1)} %bitcast.13, bf16[224,7168]{1,0:T(8,128)(2,1)S(1)} %squeeze_reshape.4, f32[]{:T(128)} %fusion.22, bf16[1,512,224]{1,2,0:T(8,128)(2,1)S(1)} %copy-done), kind=kOutput, calls=%fused_computation.9 | convolution fusion | flops 1652195328 | bytes 20414468 | tf_op jit(solution)/shard_map/dot_general | solution.py:59
  (3 shorter events, 0.0 us)
Async XLA Ops:
  7.2 467.8 %copy-start = (bf16[1,512,224]{1,2,0:T(8,128)(2,1)S(1)}, bf16[1,512,224]{1,2,0:T(8,128)(2,1)}, u32[]{:S(2)}) copy-start(bf16[1,512,224]{1,2,0:T(8,128)(2,1)} %param.7) | copy-start | bytes 688132
  43.2 10.2 %copy-start.1 = (s32[8,2]{0,1:T(2,128)S(1)}, s32[8,2]{0,1:T(2,128)}, u32[]{:S(2)}) copy-start(s32[8,2]{0,1:T(2,128)} %param.11) | copy-start | bytes 196
  43.2 154.6 %all-to-all-start = ((bf16[32,2,50176]{2,1,0:T(2,128)(2,1)}), bf16[32,2,50176]{2,1,0:T(2,128)(2,1)}, u32[]{:S(2)}, u32[]{:S(2)}) async-start(bf16[32,2,50176]{2,1,0:T(2,128)(2,1)} %reshape.74), calls=%async_computation | async-start | bytes 12845056 | tf_op jit(solution)/shard_map/all_to_all | solution.py:10
  53.3 534.5 %reduce-scatter.2.cloned.1.call-start = ((), (), s32[]{:S(2)}) async-start(), calls=%async_computation.4 | async-start | bytes 8257536 | tf_op jit(solution)/shard_map/reduce_scatter | solution.py:52
  480.1 2.3 copy-start.2
  480.1 2.9 copy-start.3
  595.4 113.4 %all-to-all-start.2 = ((bf16[8,512,896]{1,2,0:T(8,128)(2,1)}), bf16[8,512,896]{1,2,0:T(8,128)(2,1)}, u32[]{:S(2)}, u32[]{:S(2)}) async-start(bf16[8,512,896]{1,2,0:T(8,128)(2,1)} %stack.2), calls=%async_computation.3 | async-start | bytes 14680064 | tf_op jit(solution)/shard_map/all_to_all | solution.py:57
Sparse Core Ops, SparseCore 0:
  480.2 107.5 reduce-scatter.1
